TPU v7x, 32 devices: a whole 2x2x4 slice. The times are simulated.
32 devices in a mesh: row: 8 (over y, x, core), col: 4 (over z).
Axes of the slice: x: 2, y: 2, z: 4, core: 2. Of those that a mesh axis runs over, the one named last changes fastest.
Arguments:
- pair: bfloat16 [256, 256, 128], P('row', 'col'), may hold values from -6 to 6
- group: bfloat16 [32, 256, 128], P('col', 'row'), may hold values from -6 to 6
- w_query: bfloat16 [128, 128], replicated, may hold values from -0.5 to 0.5
- w_key: bfloat16 [128, 128], replicated, may hold values from -0.5 to 0.5
- w_value: bfloat16 [128, 128], replicated, may hold values from -0.5 to 0.5
- w_gate: bfloat16 [128, 128], replicated, may hold values from -0.5 to 0.5
- w_bias: float32 [128, 4], replicated, may hold values from -40 to 40
- w_out: bfloat16 [128, 128], replicated, may hold values from -0.5 to 0.5
Outputs:
- update: bfloat16 [32, 256, 128], P('col', 'row')
All inputs are finite; a program needn't handle non-finite values.
Results may differ from a plain program's by a relative error of at most 0.012.
Values may be sent and summed in bfloat16 or wider, within the bound.
No kernel may reach another device: no remote copies, remote signals or barrier semaphores. Data moves between devices by JAX's collectives and lax.ppermute only.
A program may use at most 64 MiB of HBM per device.

v0:
```python
import math
import jax
import jax.numpy as jnp
from jax import lax
from jax.sharding import PartitionSpec as P

EPS = 1e-05


def normalize(entries):
    average = jnp.mean(entries, axis=-1, keepdims=True)
    centered = entries - average
    spread = jnp.mean(centered * centered, axis=-1, keepdims=True)
    return centered * lax.rsqrt(spread + EPS)


def per_device(pair, group, w_query, w_key, w_value, w_gate, w_bias, w_out):
    head_count = w_bias.shape[1]
    proj_width = w_query.shape[1]
    head_dim = proj_width // head_count
    query_rows, pair_cols, channels = group.shape
    normed_pair = normalize(pair.astype(jnp.float32))
    bias_local = jnp.einsum("jkc,ch->hjk", normed_pair, w_bias, precision=lax.Precision.HIGHEST)
    bias_panel = lax.all_gather(bias_local, "col", axis=2, tiled=True)
    normed = normalize(group.astype(jnp.float32)).astype(jnp.bfloat16)
    flat_rows = normed.reshape(-1, channels)
    scale = 1.0 / math.sqrt(head_dim)
    query = (jnp.dot(flat_rows, w_query, preferred_element_type=jnp.float32) * scale).astype(
        jnp.bfloat16
    )
    query = query.reshape(query_rows, pair_cols, head_count, head_dim)
    gating = jax.nn.sigmoid(jnp.dot(flat_rows, w_gate, preferred_element_type=jnp.float32))
    gating = gating.reshape(query_rows, pair_cols, head_count, head_dim)
    block_rows = lax.all_gather(normed, "row", axis=1, tiled=True)
    key_count = block_rows.shape[1]
    block_flat = block_rows.reshape(-1, channels)
    key_part = jnp.dot(block_flat, w_key, preferred_element_type=jnp.float32).astype(jnp.bfloat16)
    value_part = jnp.dot(block_flat, w_value, preferred_element_type=jnp.float32).astype(
        jnp.bfloat16
    )
    key_part = key_part.reshape(query_rows, key_count, head_count, head_dim)
    value_part = value_part.reshape(query_rows, key_count, head_count, head_dim)
    run_max = jnp.full((query_rows, head_count, pair_cols), -1e30, jnp.float32)
    scores = (
        jnp.einsum("ijhd,ikhd->ihjk", query, key_part, preferred_element_type=jnp.float32)
        + bias_panel[None]
    )
    new_max = jnp.maximum(run_max, jnp.max(scores, axis=-1))
    weights = jnp.exp(scores - new_max[..., None])
    run_sum = jnp.sum(weights, axis=-1)
    mixture = jnp.einsum(
        "ihjk,ikhd->ijhd",
        weights.astype(jnp.bfloat16),
        value_part,
        preferred_element_type=jnp.float32,
    )
    accumulated = mixture
    run_max, run_sum, accumulated = (new_max, run_sum, accumulated)
    attention = accumulated / jnp.transpose(run_sum, (0, 2, 1))[..., None]
    hidden = (gating * attention).astype(jnp.bfloat16).reshape(-1, proj_width)
    result = jnp.dot(hidden, w_out, preferred_element_type=jnp.float32).astype(jnp.bfloat16)
    return result.reshape(query_rows, pair_cols, channels)


def solution(mesh):
    in_specs = (P("row", "col", None), P("col", "row", None), P(), P(), P(), P(), P(), P())
    out_specs = P("col", "row", None)
    return jax.shard_map(
        per_device, mesh=mesh, in_specs=in_specs, out_specs=out_specs, check_vma=False
    )
```

profile of v0, /device:TPU:0, one launch (start us, length us, event | category | flops | bytes accessed | tf_op | source)
XLA Modules:
  0.0 40.9 jit_solution(7191558274230785309)
XLA Ops:
  0.0 0.0 copy-start
  0.0 0.0 copy-start.2
  0.0 1.0 %convert_reduce_fusion.1 = f32[8,32]{1,0:T(8,128)S(1)} fusion(bf16[8,32,128]{2,1,0:T(8,128)(2,1)} %param.9), kind=kLoop, calls=%fused_computation.30 | loop fusion | flops 65280 | bytes 66560 | tf_op jit(solution)/shard_map/reduce_sum | solution.py:11
  1.0 0.0 copy-done.2
  1.0 0.2 fusion.22
  1.2 0.1 fusion.23
  1.4 11.3 %all_gather.6 = bf16[8,256,128]{2,1,0:T(8,128)(2,1)S(1)} all-gather(bf16[8,32,128]{2,1,0:T(8,128)(2,1)S(1)} %fusion.23), channel_id=1, replica_groups=mesh['row'=8,'col'=4] {'row'}, dimensions={1}, use_global_device_ids=true | all-gather | bytes 589824 | tf_op jit(solution)/shard_map/all_gather | solution.py:34
  12.7 0.0 copy-done
  12.7 0.3 convolution_convert_fusion
  13.0 0.2 copy.23
  13.2 0.0 copy-start.3
  13.2 0.0 copy-start.1
  13.3 0.1 copy.32
  13.4 0.6 %copy-done.3 = bf16[128,128]{1,0:T(8,128)(2,1)S(1)} copy-done((bf16[128,128]{1,0:T(8,128)(2,1)S(1)}, bf16[128,128]{1,0:T(8,128)(2,1)}, u32[]{:S(2)}) %copy-start.3) | copy-done | bytes 32792
  14.0 0.1 fusion.8
  14.1 0.2 reshape.57
  14.3 0.0 copy-done.1
  14.3 0.3 convert_reduce_fusion
  14.7 0.6 %fusion.9 = f32[32,64]{1,0:T(8,128)S(1)} fusion(bf16[32,64,128]{2,1,0:T(8,128)(2,1)S(1)} %copy-done.1, f32[32,64]{1,0:T(8,128)S(1)} %broadcast_multiply_fusion), kind=kLoop, calls=%fused_computation.19 | loop fusion | flops 1046528 | bytes 540672 | tf_op jit(solution)/shard_map/reduce_sum | solution.py:13
  15.3 0.0 copy-start.7
  15.4 0.7 %copy-done.7 = f32[128,4]{0,1:T(4,128)S(1)} copy-done((f32[128,4]{0,1:T(4,128)S(1)}, f32[128,4]{0,1:T(4,128)}, u32[]{:S(2)}) %copy-start.7) | copy-done | bytes 2072
  16.0 2.9 %convolution_bitcast_fusion.1 = f32[4,32,64]{2,0,1:T(4,128)S(1)} fusion(bf16[32,64,128]{2,1,0:T(8,128)(2,1)S(1)} %copy-done.1, f32[32,64]{1,0:T(8,128)S(1)} %add_rsqrt_fusion, f32[32,64]{1,0:T(8,128)S(1)} %broadcast_multiply_fusion, f32[128,4]{0,1:T(4,128)S(1)} %copy-done.7), kind=kOutput, calls=%fused_computation.18 | convolution fusion | flops 13369344 | bytes 575488 | tf_op jit(solution)/shard_map/jkc,ch->hjk/dot_general | solution.py:23
  18.9 0.1 copy.26
  19.1 16.3 %all_gather.7 = f32[4,32,256]{1,0,2:T(4,128)S(1)} all-gather(f32[4,32,64]{1,0,2:T(4,128)S(1)} %copy.26), channel_id=1, replica_groups=mesh['row'=8,'col'=4] {'col'}, dimensions={2}, use_global_device_ids=true | all-gather | bytes 163840 | tf_op jit(solution)/shard_map/all_gather | solution.py:24
  35.4 0.2 copy.27
  35.6 0.4 fusion.25
  36.0 0.0 copy-start.4
  36.0 0.4 %fusion.11 = f32[8,4,32]{2,1,0:T(4,128)S(1)} fusion(f32[8,4,32,256]{3,2,1,0:T(8,128)S(1)} %get-tuple-element.6, f32[8,4,32]{2,1,0:T(4,128)S(1)} %broadcast_maximum_fusion), kind=kLoop, calls=%fused_computation.21 | loop fusion | flops 523264 | bytes 1056768 | tf_op jit(solution)/shard_map/reduce_sum | solution.py:50
  36.4 0.3 copy-done.4
  36.8 0.3 convolution_convert_fusion.1
  37.0 0.2 copy.22
  37.3 0.0 copy-start.6
  37.3 0.1 copy.31
  37.4 0.6 %copy-done.6 = bf16[128,128]{1,0:T(8,128)(2,1)S(1)} copy-done((bf16[128,128]{1,0:T(8,128)(2,1)S(1)}, bf16[128,128]{1,0:T(8,128)(2,1)}, u32[]{:S(2)}) %copy-start.6) | copy-done | bytes 32792
  38.0 0.2 fusion.7
  38.2 0.3 reshape.54
  38.5 0.2 copy.29
  38.7 0.4 fusion.4
  39.1 0.2 copy.30
  39.3 0.0 copy-start.5
  39.3 0.2 reshape.59
  39.5 0.6 %copy-done.5 = bf16[128,128]{1,0:T(8,128)(2,1)S(1)} copy-done((bf16[128,128]{1,0:T(8,128)(2,1)S(1)}, bf16[128,128]{1,0:T(8,128)(2,1)}, u32[]{:S(2)}) %copy-start.5) | copy-done | bytes 32792
  40.0 0.8 %convolution_convert_fusion.2 = bf16[256,128]{1,0:T(8,128)(2,1)} fusion(bf16[256,128]{0,1:T(8,128)(2,1)S(1)} %reshape.59, bf16[128,128]{1,0:T(8,128)(2,1)S(1)} %copy-done.5), kind=kOutput, calls=%fused_computation.16 | convolution fusion | flops 8421376 | bytes 163840 | tf_op jit(solution)/shard_map/dot_general | solution.py:61
  (5 shorter events, 0.0 us)
Async XLA Ops:
  0.0 12.7 %copy-start = (bf16[128,128]{1,0:T(8,128)(2,1)S(1)}, bf16[128,128]{1,0:T(8,128)(2,1)}, u32[]{:S(2)}) copy-start(bf16[128,128]{1,0:T(8,128)(2,1)} %param.11) | copy-start | bytes 98308
  0.0 1.0 %copy-start.2 = (bf16[8,32,128]{2,1,0:T(8,128)(2,1)S(1)}, bf16[8,32,128]{2,1,0:T(8,128)(2,1)}, u32[]{:S(2)}) copy-start(bf16[8,32,128]{2,1,0:T(8,128)(2,1)} %param.9) | copy-start | bytes 196612
  13.2 0.8 %copy-start.3 = (bf16[128,128]{1,0:T(8,128)(2,1)S(1)}, bf16[128,128]{1,0:T(8,128)(2,1)}, u32[]{:S(2)}) copy-start(bf16[128,128]{1,0:T(8,128)(2,1)} %param.10) | copy-start | bytes 98308
  13.2 1.1 %copy-start.1 = (bf16[32,64,128]{2,1,0:T(8,128)(2,1)S(1)}, bf16[32,64,128]{2,1,0:T(8,128)(2,1)}, u32[]{:S(2)}) copy-start(bf16[32,64,128]{2,1,0:T(8,128)(2,1)} %param.8) | copy-start | bytes 1572868
  15.3 0.7 %copy-start.7 = (f32[128,4]{0,1:T(4,128)S(1)}, f32[128,4]{0,1:T(4,128)}, u32[]{:S(2)}) copy-start(f32[128,4]{0,1:T(4,128)} %param.14) | copy-start | bytes 6148
  36.0 0.8 %copy-start.4 = (bf16[128,128]{1,0:T(8,128)(2,1)S(1)}, bf16[128,128]{1,0:T(8,128)(2,1)}, u32[]{:S(2)}) copy-start(bf16[128,128]{1,0:T(8,128)(2,1)} %param.12) | copy-start | bytes 98308
  37.3 0.8 %copy-start.6 = (bf16[128,128]{1,0:T(8,128)(2,1)S(1)}, bf16[128,128]{1,0:T(8,128)(2,1)}, u32[]{:S(2)}) copy-start(bf16[128,128]{1,0:T(8,128)(2,1)} %param.13) | copy-start | bytes 98308
  39.3 0.8 %copy-start.5 = (bf16[128,128]{1,0:T(8,128)(2,1)S(1)}, bf16[128,128]{1,0:T(8,128)(2,1)}, u32[]{:S(2)}) copy-start(bf16[128,128]{1,0:T(8,128)(2,1)} %param.15) | copy-start | bytes 98308
where the time goes:
time: 41.3 us; the launch traced here: 40.9 us
  blocking collectives  27.7 us (67%)
  matrix products  5.42 us (13%)
  local copies, waits for them, and re-layouts  4.77 us (12%)
  other arithmetic  2.76 us (7%)
    all_gather x1, blocking collectives, per_device(): bias_panel = lax.all_gather(bias_local, 'col', axis=2, tiled=True)  16.3 us
    all_gather x1, blocking collectives, per_device(): block_rows = lax.all_gather(normed, 'row', axis=1, tiled=True)  11.3 us
    unnamed x18, local copies, waits for them, and re-layouts  3.06 us
    dot_general x1, matrix products, per_device(): jnp.einsum('jkc,ch->hjk', normed_pair, w_bias, precision=lax.Precision.HI...  2.93 us
    reduce_sum x2, other arithmetic, normalize(): average = jnp.mean(entries, axis=-1, keepdims=True)  1.35 us

commit v1 on v0

--- a/solution.py
+++ b/solution.py
@@ -21,7 +21,12 @@
     query_rows, pair_cols, channels = group.shape
     normed_pair = normalize(pair.astype(jnp.float32))
     bias_local = jnp.einsum("jkc,ch->hjk", normed_pair, w_bias, precision=lax.Precision.HIGHEST)
-    bias_panel = lax.all_gather(bias_local, "col", axis=2, tiled=True)
+    ring = [bias_local]
+    for hop in range(3):
+        ring.append(lax.ppermute(ring[-1], "col", [(dev, (dev + 1) % 4) for dev in range(4)]))
+    bias_panel = jnp.roll(
+        jnp.concatenate(ring[::-1], axis=2), (lax.axis_index("col") + 1) * ring[0].shape[2], axis=2
+    )
     normed = normalize(group.astype(jnp.float32)).astype(jnp.bfloat16)
     flat_rows = normed.reshape(-1, channels)
     scale = 1.0 / math.sqrt(head_dim)

time: 41.3 us -> 36.4 us (0.88)
  blocking collectives: 27.7 us -> 9.86 us
  waiting for transfers between devices: 0 us -> 8.96 us
  starting transfers between devices: 0 us -> 4.7 us
  local copies, waits for them, and re-layouts: 4.77 us -> 3.85 us
    all_gather x1 -> x0, blocking collectives: 16.3 us -> none  [per_device(): bias_panel = lax.all_gather(bias_local, 'col', axis=2, tiled=True)]
    ppermute x0 -> x3, waiting for transfers between devices: none -> 8.96 us  [per_device(): lax.ppermute(ring[-1], 'col', [(dev, (dev + 1) % 4) for dev in range(4)])]
    ppermute x0 -> x3, starting transfers between devices: none -> 4.7 us  [per_device(): lax.ppermute(ring[-1], 'col', [(dev, (dev + 1) % 4) for dev in range(4)])]
    all_gather x1, blocking collectives: 11.3 us -> 9.86 us  [per_device(): block_rows = lax.all_gather(normed, 'row', axis=1, tiled=True)]
    unnamed x18, local copies, waits for them, and re-layouts: 3.06 us -> 1.95 us
  transfers between devices with their start and end apart: 0 -> 3, of which waited for: 0 -> 2; matrix products, arithmetic and copies ran while one was open for 0% -> 7% of each run, Pallas kernels for 0% -> 0%
where the time goes in v1:
time: 36.4 us; the launch traced here: 36.1 us
  blocking collectives  9.86 us (27%)
  waiting for transfers between devices  8.96 us (25%)
  matrix products  5.47 us (15%)
  starting transfers between devices  4.7 us (13%)
  local copies, waits for them, and re-layouts  3.85 us (11%)
  other arithmetic  2.99 us (8%)
    all_gather x1, blocking collectives, per_device(): block_rows = lax.all_gather(normed, 'row', axis=1, tiled=True)  9.86 us
    ppermute x3, waiting for transfers between devices, per_device(): lax.ppermute(ring[-1], 'col', [(dev, (dev + 1) % 4) for dev in range(4)])  8.96 us
    ppermute x3, starting transfers between devices, per_device(): lax.ppermute(ring[-1], 'col', [(dev, (dev + 1) % 4) for dev in range(4)])  4.7 us
    dot_general x1, matrix products, per_device(): jnp.einsum('jkc,ch->hjk', normed_pair, w_bias, precision=lax.Precision.HI...  2.93 us
    unnamed x18, local copies, waits for them, and re-layouts  1.95 us
    reduce_sum x2, other arithmetic, normalize(): average = jnp.mean(entries, axis=-1, keepdims=True)  1.56 us
    dot_general x1, matrix products, per_device(): jnp.dot(hidden, w_out, preferred_element_type=jnp.float32)  0.82 us
    reduce_sum x2, other arithmetic, normalize(): spread = jnp.mean(centered * centered, axis=-1, keepdims=True)  0.82 us
  transfers between devices with their start and end apart: 3, of which 2 were waited for; matrix products, arithmetic and copies ran while one was open for 7% of the time, Pallas kernels for 0%

profile of v1, /device:TPU:0, one launch (start us, length us, event | category | flops | bytes accessed | tf_op | source)
XLA Modules:
  0.0 36.1 jit_solution(15259412189736184466)
XLA Ops:
  0.0 0.0 copy-start
  0.0 0.0 copy-start.1
  0.0 1.5 %convert_reduce_fusion = f32[32,64]{1,0:T(8,128)S(1)} fusion(bf16[32,64,128]{2,1,0:T(8,128)(2,1)} %param.8), kind=kLoop, calls=%fused_computation.3 | loop fusion | flops 522240 | bytes 532480 | tf_op jit(solution)/shard_map/reduce_sum | solution.py:11
  1.5 0.0 copy-done.1
  1.5 0.6 %fusion.9 = f32[32,64]{1,0:T(8,128)S(1)} fusion(bf16[32,64,128]{2,1,0:T(8,128)(2,1)S(1)} %copy-done.1, f32[32,64]{1,0:T(8,128)S(1)} %broadcast_multiply_fusion), kind=kLoop, calls=%fused_computation.18 | loop fusion | flops 1046528 | bytes 540672 | tf_op jit(solution)/shard_map/reduce_sum | solution.py:13
  2.1 0.0 copy-start.7
  2.2 0.7 %copy-done.7 = f32[128,4]{0,1:T(4,128)S(1)} copy-done((f32[128,4]{0,1:T(4,128)S(1)}, f32[128,4]{0,1:T(4,128)}, u32[]{:S(2)}) %copy-start.7) | copy-done | bytes 2072
  2.8 0.0 copy-start.2
  2.8 2.9 %convolution_bitcast_fusion.1 = f32[4,32,64]{2,0,1:T(4,128)S(1)} fusion(bf16[32,64,128]{2,1,0:T(8,128)(2,1)S(1)} %copy-done.1, f32[32,64]{1,0:T(8,128)S(1)} %add_rsqrt_fusion, f32[32,64]{1,0:T(8,128)S(1)} %broadcast_multiply_fusion, f32[128,4]{0,1:T(4,128)S(1)} %copy-done.7), kind=kOutput, calls=%fused_computation.17 | convolution fusion | flops 13369344 | bytes 575488 | tf_op jit(solution)/shard_map/jkc,ch->hjk/dot_general | solution.py:23
  5.8 3.1 %collective-permute-start = (f32[4,32,64]{2,0,1:T(4,128)S(1)}, f32[4,32,64]{2,0,1:T(4,128)S(1)}, u32[]{:S(2)}, u32[]{:S(2)}) collective-permute-start(f32[4,32,64]{2,0,1:T(4,128)S(1)} %convolution_bitcast_fusion.1), channel_id=1, source_target_pairs={{0,1},{1,2},{2,3},{3,0},{4,5},{5,6},{6,7},{7,4},{8,9},{9,10},{10,1... | collective-permute-start | bytes 98312 | tf_op jit(solution)/shard_map/ppermute | solution.py:26
  8.8 0.0 copy-done.2
  8.8 0.1 convert_reduce_fusion.1
  8.9 0.2 fusion.24
  9.1 0.1 fusion.25
  9.3 9.9 %all_gather.3 = bf16[8,256,128]{2,1,0:T(8,128)(2,1)S(1)} all-gather(bf16[8,32,128]{2,1,0:T(8,128)(2,1)S(1)} %fusion.25), channel_id=1, replica_groups=mesh['row'=8,'col'=4] {'row'}, dimensions={1}, use_global_device_ids=true | all-gather | bytes 589824 | tf_op jit(solution)/shard_map/all_gather | solution.py:39
  19.1 0.0 copy-done
  19.1 0.0 copy-start.3
  19.2 0.3 convolution_convert_fusion
  19.4 0.5 %copy-done.3 = bf16[128,128]{1,0:T(8,128)(2,1)S(1)} copy-done((bf16[128,128]{1,0:T(8,128)(2,1)S(1)}, bf16[128,128]{1,0:T(8,128)(2,1)}, u32[]{:S(2)}) %copy-start.3) | copy-done | bytes 32792
  19.9 0.0 copy-start.6
  19.9 0.3 convolution_convert_fusion.1
  20.2 0.0 collective-permute-done
  20.2 1.6 %collective-permute-start.1 = (f32[4,32,64]{2,0,1:T(4,128)S(1)}, f32[4,32,64]{2,0,1:T(4,128)S(1)}, u32[]{:S(2)}, u32[]{:S(2)}) collective-permute-start(f32[4,32,64]{2,0,1:T(4,128)S(1)} %collective-permute-done), channel_id=1, source_target_pairs={{0,1},{1,2},{2,3},{3,0},{4,5},{5,6},{6,7},{7,4},{8,9},{9,10},{10,1... | collective-permute-start | bytes 98312 | tf_op jit(solution)/shard_map/ppermute | solution.py:26
  21.8 0.0 copy-done.6
  21.8 0.0 copy-start.4
  21.8 0.2 fusion.7
  22.0 4.4 %collective-permute-done.1 = f32[4,32,64]{2,0,1:T(4,128)S(1)} collective-permute-done((f32[4,32,64]{2,0,1:T(4,128)S(1)}, f32[4,32,64]{2,0,1:T(4,128)S(1)}, u32[]{:S(2)}, u32[]{:S(2)}) %collective-permute-start.1) | collective-permute-done | bytes 32800 | tf_op jit(solution)/shard_map/ppermute | solution.py:26
  26.4 0.0 collective-permute-start.2
  26.4 0.0 copy-done.4
  26.4 0.1 fusion.8
  26.6 0.2 copy.15
  26.8 0.1 copy.23
  26.9 0.2 reshape.57
  27.1 0.2 copy.14
  27.3 0.1 copy.22
  27.4 0.3 reshape.54
  27.7 0.2 copy.20
  27.9 4.6 %collective-permute-done.2 = f32[4,32,64]{2,0,1:T(4,128)S(1)} collective-permute-done((f32[4,32,64]{2,0,1:T(4,128)S(1)}, f32[4,32,64]{2,0,1:T(4,128)S(1)}, u32[]{:S(2)}, u32[]{:S(2)}) %collective-permute-start.2) | collective-permute-done | bytes 32800 | tf_op jit(solution)/shard_map/ppermute | solution.py:26
  32.5 0.3 concatenate.6
  32.8 0.1 constant_dynamic-slice_fusion
  33.0 0.4 %add_reduce_fusion = (f32[8,4,32]{2,1,0:T(4,128)S(1)}, f32[8,4,32,256]{3,2,1,0:T(8,128)S(1)}) fusion(f32[4,32,256]{2,1,0:T(8,128)S(1)} %copy.18, bf16[8,256,4,32]{1,0,3,2:T(8,128)(2,1)S(1)} %bitcast.45, bf16[8,32,4,32]{3,2,1,0:T(4,128)(2,1)S(1)} %reshape.57), kind=kOutput, calls=%fused_computation.20 | convolution fusion | flops 17300480 | bytes 1773568 | tf_op jit(solution)/shard_map/ijhd,ikhd->ihjk/dot_general | solution.py:50
  33.4 0.5 %fusion.11 = f32[8,4,32]{2,1,0:T(4,128)S(1)} fusion(f32[8,4,32,256]{3,2,1,0:T(8,128)S(1)} %get-tuple-element.6, f32[8,4,32]{2,1,0:T(4,128)S(1)} %broadcast_maximum_fusion, f32[4,32,256]{2,1,0:T(8,128)S(1)} %copy.18), kind=kLoop, calls=%fused_computation.21 | loop fusion | flops 785408 | bytes 1187840 | tf_op jit(solution)/shard_map/reduce_sum | solution.py:55
  33.9 0.4 %fusion.4 = bf16[8,32,4,32]{1,3,2,0:T(8,128)(2,1)S(1)} fusion(f32[8,32,4,32]{1,3,2,0:T(8,128)S(1)} %copy.20, f32[8,4,32,256]{3,2,1,0:T(8,128)S(1)} %get-tuple-element.6, bf16[8,256,4,32]{1,0,3,2:T(8,128)(2,1)S(1)} %bitcast.48, f32[8,4,32]{2,1,0:T(4,128)S(1)} %broadcast_maximum_fusion, f32[4,32,256]{2,1,0:T(8,128)S(1)} %copy.18, f32[8,32,4]{1,2,0:T(4,128)S(1)} %bitcast.49), kind=kOutput, calls=%fused_computation.9 | convolution fusion | flops 17661952 | bytes 1908736 | tf_op jit(solution)/shard_map/ihjk,ikhd->ijhd/dot_general | solution.py:56
  34.3 0.2 copy.21
  34.5 0.0 copy-start.5
  34.5 0.2 reshape.59
  34.7 0.6 %copy-done.5 = bf16[128,128]{1,0:T(8,128)(2,1)S(1)} copy-done((bf16[128,128]{1,0:T(8,128)(2,1)S(1)}, bf16[128,128]{1,0:T(8,128)(2,1)}, u32[]{:S(2)}) %copy-start.5) | copy-done | bytes 32792
  35.3 0.8 %convolution_convert_fusion.2 = bf16[256,128]{1,0:T(8,128)(2,1)} fusion(bf16[256,128]{0,1:T(8,128)(2,1)S(1)} %reshape.59, bf16[128,128]{1,0:T(8,128)(2,1)S(1)} %copy-done.5), kind=kOutput, calls=%fused_computation.15 | convolution fusion | flops 8421376 | bytes 163840 | tf_op jit(solution)/shard_map/dot_general | solution.py:66
  (6 shorter events, 0.1 us)
Async XLA Ops:
  0.0 19.1 %copy-start = (bf16[128,128]{1,0:T(8,128)(2,1)S(1)}, bf16[128,128]{1,0:T(8,128)(2,1)}, u32[]{:S(2)}) copy-start(bf16[128,128]{1,0:T(8,128)(2,1)} %param.11) | copy-start | bytes 98308
  0.0 1.5 %copy-start.1 = (bf16[32,64,128]{2,1,0:T(8,128)(2,1)S(1)}, bf16[32,64,128]{2,1,0:T(8,128)(2,1)}, u32[]{:S(2)}) copy-start(bf16[32,64,128]{2,1,0:T(8,128)(2,1)} %param.8) | copy-start | bytes 1572868
  2.1 0.7 %copy-start.7 = (f32[128,4]{0,1:T(4,128)S(1)}, f32[128,4]{0,1:T(4,128)}, u32[]{:S(2)}) copy-start(f32[128,4]{0,1:T(4,128)} %param.14) | copy-start | bytes 6148
  2.8 6.0 %copy-start.2 = (bf16[8,32,128]{2,1,0:T(8,128)(2,1)S(1)}, bf16[8,32,128]{2,1,0:T(8,128)(2,1)}, u32[]{:S(2)}) copy-start(bf16[8,32,128]{2,1,0:T(8,128)(2,1)} %param.9) | copy-start | bytes 196612
  5.8 14.4 %collective-permute-start = (f32[4,32,64]{2,0,1:T(4,128)S(1)}, f32[4,32,64]{2,0,1:T(4,128)S(1)}, u32[]{:S(2)}, u32[]{:S(2)}) collective-permute-start(f32[4,32,64]{2,0,1:T(4,128)S(1)} %convolution_bitcast_fusion.1), channel_id=1, source_target_pairs={{0,1},{1,2},{2,3},{3,0},{4,5},{5,6},{6,7},{7,4},{8,9},{9,10},{10,1... | collective-permute-start | bytes 98312 | tf_op jit(solution)/shard_map/ppermute | solution.py:26
  19.1 0.8 %copy-start.3 = (bf16[128,128]{1,0:T(8,128)(2,1)S(1)}, bf16[128,128]{1,0:T(8,128)(2,1)}, u32[]{:S(2)}) copy-start(bf16[128,128]{1,0:T(8,128)(2,1)} %param.12) | copy-start | bytes 98308
  19.9 1.9 %copy-start.6 = (bf16[128,128]{1,0:T(8,128)(2,1)S(1)}, bf16[128,128]{1,0:T(8,128)(2,1)}, u32[]{:S(2)}) copy-start(bf16[128,128]{1,0:T(8,128)(2,1)} %param.13) | copy-start | bytes 98308
  20.2 6.2 %collective-permute-start.1 = (f32[4,32,64]{2,0,1:T(4,128)S(1)}, f32[4,32,64]{2,0,1:T(4,128)S(1)}, u32[]{:S(2)}, u32[]{:S(2)}) collective-permute-start(f32[4,32,64]{2,0,1:T(4,128)S(1)} %collective-permute-done), channel_id=1, source_target_pairs={{0,1},{1,2},{2,3},{3,0},{4,5},{5,6},{6,7},{7,4},{8,9},{9,10},{10,1... | collective-permute-start | bytes 98312 | tf_op jit(solution)/shard_map/ppermute | solution.py:26
  21.8 4.6 %copy-start.4 = (bf16[128,128]{1,0:T(8,128)(2,1)S(1)}, bf16[128,128]{1,0:T(8,128)(2,1)}, u32[]{:S(2)}) copy-start(bf16[128,128]{1,0:T(8,128)(2,1)} %param.10) | copy-start | bytes 98308
  26.4 6.1 %collective-permute-start.2 = (f32[4,32,64]{2,0,1:T(4,128)S(1)}, f32[4,32,64]{2,0,1:T(4,128)S(1)}, u32[]{:S(2)}, u32[]{:S(2)}) collective-permute-start(f32[4,32,64]{2,0,1:T(4,128)S(1)} %collective-permute-done.1), channel_id=1, source_target_pairs={{0,1},{1,2},{2,3},{3,0},{4,5},{5,6},{6,7},{7,4},{8,9},{9,10},{10,1... | collective-permute-start | bytes 98312 | tf_op jit(solution)/shard_map/ppermute | solution.py:26
  34.5 0.8 %copy-start.5 = (bf16[128,128]{1,0:T(8,128)(2,1)S(1)}, bf16[128,128]{1,0:T(8,128)(2,1)}, u32[]{:S(2)}) copy-start(bf16[128,128]{1,0:T(8,128)(2,1)} %param.15) | copy-start | bytes 98308
